TPU v7x, 32 devices: a whole 2x2x4 slice. The times are simulated.
32 devices in a mesh: dp: 4 (over y, x), fsdp: 8 (over z, core).
Axes of the slice: x: 2, y: 2, z: 4, core: 2. Of those that a mesh axis runs over, the one named last changes fastest.
Arguments:
- hidden_in: bfloat16 [32, 8192], P(('dp', 'fsdp')), may hold values from -6 to 6
- lengths: int32 [32], P(('dp', 'fsdp')), may hold values from 1 to 511
- key_cache: bfloat16 [32, 512, 1024], P(('dp', 'fsdp')), may hold values from -68 to 68
- value_cache: bfloat16 [32, 512, 1024], P(('dp', 'fsdp')), may hold values from -6 to 6
- attn_gain: bfloat16 [8192], replicated, may hold values from 0.5 to 1.5
- w_qkv: bfloat16 [8192, 10240], P('fsdp', 'dp'), may hold values from -0.0625 to 0.0625
- w_out: bfloat16 [8192, 8192], P('fsdp', 'dp'), may hold values from -0.5 to 0.5
- mlp_gain: bfloat16 [8192], replicated, may hold values from 0.5 to 1.5
- w_gate: bfloat16 [8192, 28672], P('dp', 'fsdp'), may hold values from -0.0625 to 0.0625
- w_up: bfloat16 [8192, 28672], P('dp', 'fsdp'), may hold values from -0.0625 to 0.0625
- w_down: bfloat16 [28672, 8192], P('fsdp', 'dp'), may hold values from -0.03125 to 0.03125
Outputs:
- hidden_out: bfloat16 [32, 8192], P(('dp', 'fsdp'))
- new_keys: bfloat16 [32, 1024], P(('dp', 'fsdp'))
- new_values: bfloat16 [32, 1024], P(('dp', 'fsdp'))
Inputs may be any that keep to these rules, and one draw needn't show every extreme that they name: Each sequence's number of cached positions; its new token takes position lengths.
All inputs are finite; a program needn't handle non-finite values.
Results may differ from a plain program's by a relative error of at most 0.012.
The roundings to bfloat16 on the way count: a program that leaves them out, or rounds other values in their place, can miss the bound.
Values may be sent and summed in bfloat16 or wider, within the bound.
A program may use at most 128 MiB of HBM per device.

v0:
```python
import jax
import jax.numpy as jnp
from jax import lax
from jax.sharding import PartitionSpec as P

HEADS = 64
KV_HEADS = 8
HD = 128


rope_base = 500000.0
norm_eps = 1e-05


def rms_scale(values, gain_row):
    mean_square = jnp.mean(values * values, axis=-1, keepdims=True)
    return values * lax.rsqrt(mean_square + norm_eps) * gain_row.astype(jnp.float32)


def rotate(values, positions):
    half_dim = values.shape[-1] // 2
    frequency = rope_base ** (-2.0 * jnp.arange(half_dim, dtype=jnp.float32) / values.shape[-1])
    angles = positions.astype(jnp.float32)[:, None] * frequency[None, :]
    cosine = jnp.cos(angles)[:, None, :]
    sine_wave = jnp.sin(angles)[:, None, :]
    lower_half = values[..., :half_dim]
    upper_half = values[..., half_dim:]
    return jnp.concatenate(
        [
            lower_half * cosine - upper_half * sine_wave,
            upper_half * cosine + lower_half * sine_wave,
        ],
        axis=-1,
    )


def attend(queries, new_keys, new_values, key_cache, value_cache, lengths):
    seq_count, context, kv_width = key_cache.shape
    kv_heads = new_keys.shape[1]
    head_dim = new_keys.shape[2]
    score_scale = head_dim ** (-0.5)
    key_rows = key_cache.reshape(seq_count, context, kv_heads, head_dim)
    value_rows = value_cache.reshape(seq_count, context, kv_heads, head_dim)
    grouped = queries.reshape(seq_count, kv_heads, -1, head_dim)
    scores = (
        jnp.einsum("skgd,sckd->skgc", grouped, key_rows, preferred_element_type=jnp.float32)
        * score_scale
    )
    is_valid = (
        jnp.arange(context, dtype=jnp.int32)[None, None, None, :] < lengths[:, None, None, None]
    )
    scores = jnp.where(is_valid, scores, -1e30)
    own_score = (
        jnp.einsum("skgd,skd->skg", grouped, new_keys, preferred_element_type=jnp.float32)
        * score_scale
    )
    row_max = jnp.maximum(jnp.max(scores, axis=-1), own_score)
    weights = jnp.exp(scores - row_max[..., None])
    own_weight = jnp.exp(own_score - row_max)
    denom_sum = jnp.sum(weights, axis=-1) + own_weight
    probability = (weights / denom_sum[..., None]).astype(jnp.bfloat16)
    own_prob = (own_weight / denom_sum).astype(jnp.bfloat16)
    mixed = jnp.einsum(
        "skgc,sckd->skgd", probability, value_rows, preferred_element_type=jnp.float32
    )
    mixed = (
        mixed
        + own_prob.astype(jnp.float32)[..., None] * new_values.astype(jnp.float32)[:, :, None, :]
    )
    return mixed.astype(jnp.bfloat16).reshape(seq_count, -1)


def quarter_split(values, dp_size, fsdp_size):
    seq_count = values.shape[0]
    return values.reshape(seq_count, fsdp_size, dp_size, -1)


def quarter_join(moved, dp_size):
    return moved.reshape(dp_size, moved.shape[0] // dp_size, -1)[None]


def on_device(
    hidden_in,
    lengths,
    key_cache,
    value_cache,
    attn_gain,
    w_qkv,
    w_out,
    mlp_gain,
    w_gate,
    w_up,
    w_down,
):
    seq_count = hidden_in.shape[0]
    q_width = HEADS * HD
    kv_width = KV_HEADS * HD
    dp_size = lax.axis_size("dp")
    fsdp_size = lax.axis_size("fsdp")
    residual = hidden_in.astype(jnp.float32)
    normed = rms_scale(residual, attn_gain).astype(jnp.bfloat16)
    qkv_tile = lax.all_to_all(
        lax.all_to_all(w_qkv, "dp", split_axis=0, concat_axis=1, tiled=True),
        "fsdp",
        split_axis=1,
        concat_axis=0,
        tiled=True,
    )
    qkv_moved = lax.all_to_all(
        quarter_split(normed, dp_size, fsdp_size), "dp", split_axis=2, concat_axis=0, tiled=True
    )
    qkv_in = quarter_join(qkv_moved, dp_size)
    qkv_parts = jnp.einsum(
        "fpsk,kn->fpsn",
        lax.all_gather(qkv_in, "fsdp", axis=0, tiled=True),
        qkv_tile,
        preferred_element_type=jnp.float32,
    )
    qkv_share = lax.psum_scatter(qkv_parts, "dp", scatter_dimension=1, tiled=True)
    projected = lax.all_to_all(qkv_share, "fsdp", split_axis=0, concat_axis=3, tiled=True)[0, 0]
    queries = rotate(projected[:, :q_width].reshape(seq_count, HEADS, HD), lengths).astype(
        jnp.bfloat16
    )
    new_keys = rotate(
        projected[:, q_width : q_width + kv_width].reshape(seq_count, KV_HEADS, HD), lengths
    ).astype(jnp.bfloat16)
    new_values = projected[:, q_width + kv_width :].astype(jnp.bfloat16)
    mixed = attend(
        queries,
        new_keys,
        new_values.reshape(seq_count, KV_HEADS, HD),
        key_cache,
        value_cache,
        lengths,
    )
    out_tile = lax.all_to_all(
        lax.all_to_all(w_out, "dp", split_axis=0, concat_axis=1, tiled=True),
        "fsdp",
        split_axis=1,
        concat_axis=0,
        tiled=True,
    )
    out_moved = lax.all_to_all(
        quarter_split(mixed, dp_size, fsdp_size), "dp", split_axis=2, concat_axis=0, tiled=True
    )
    out_in = quarter_join(out_moved, dp_size)
    out_parts = jnp.einsum(
        "fpsk,kn->fpsn",
        lax.all_gather(out_in, "fsdp", axis=0, tiled=True),
        out_tile,
        preferred_element_type=jnp.float32,
    )
    out_share = lax.psum_scatter(out_parts, "dp", scatter_dimension=1, tiled=True)
    attn_sum = lax.all_to_all(out_share, "fsdp", split_axis=0, concat_axis=3, tiled=True)[0, 0]
    residual_mid = residual + attn_sum
    normed_mid = rms_scale(residual_mid, mlp_gain).astype(jnp.bfloat16)
    mlp_in = lax.all_to_all(normed_mid[None], "dp", split_axis=2, concat_axis=0, tiled=True)
    pieces = lax.all_gather(mlp_in[None], "fsdp", axis=0, tiled=True)
    gate_part = jnp.einsum("fask,kn->fasn", pieces, w_gate, preferred_element_type=jnp.float32)
    up_part = jnp.einsum("fask,kn->fasn", pieces, w_up, preferred_element_type=jnp.float32)
    partials = jnp.stack([gate_part, up_part], axis=3)
    summed = lax.psum(partials.astype(jnp.bfloat16), "dp").astype(jnp.float32)
    activated = (jax.nn.silu(summed[:, :, :, 0]) * summed[:, :, :, 1]).astype(jnp.bfloat16)
    reduced_down = lax.psum_scatter(
        jnp.einsum("fask,kn->fasn", activated, w_down, preferred_element_type=jnp.float32),
        "fsdp",
        scatter_dimension=0,
        tiled=True,
    )
    down_sum = lax.all_to_all(
        reduced_down.astype(jnp.bfloat16), "dp", split_axis=1, concat_axis=3, tiled=True
    ).astype(reduced_down.dtype)[0, 0]
    hidden_out = (residual_mid + down_sum).astype(jnp.bfloat16)
    return (hidden_out, new_keys.reshape(seq_count, kv_width), new_values)


def solution(mesh):
    in_specs = (
        P(("dp", "fsdp"), None),
        P(("dp", "fsdp")),
        P(("dp", "fsdp"), None, None),
        P(("dp", "fsdp"), None, None),
        P(),
        P("fsdp", "dp"),
        P("fsdp", "dp"),
        P(),
        P("dp", "fsdp"),
        P("dp", "fsdp"),
        P("fsdp", "dp"),
    )
    out_specs = (P(("dp", "fsdp"), None), P(("dp", "fsdp"), None), P(("dp", "fsdp"), None))
    return jax.shard_map(
        on_device, mesh=mesh, in_specs=in_specs, out_specs=out_specs, check_vma=False
    )
```

profile of v0, /device:TPU:0, one launch (start us, length us, event | category | flops | bytes accessed | tf_op | source)
XLA Modules:
  0.0 717.8 jit_solution(7056581813542173455)
XLA Ops:
  7.2 5.3 all-to-all-start.1
  12.5 0.7 multiply_reduce_fusion.1
  13.9 0.1 convert_reduce_fusion
  14.0 0.6 copy.50
  14.6 57.9 %all-to-all-done.1 = bf16[4,256,2560]{2,1,0:T(8,128)(2,1)} async-done(((bf16[4,256,2560]{2,1,0:T(8,128)(2,1)}), bf16[4,256,2560]{2,1,0:T(8,128)(2,1)}, u32[]{:S(2)}, u32[]{:S(2)}) %all-to-all-start.1) | async-done | bytes 5242912 | tf_op jit(solution)/shard_map/all_to_all | solution.py:103
  72.5 3.3 all-to-all-start
  75.8 8.0 %copy.52 = bf16[256,4,2560]{0,2,1:T(8,128)(2,1)} copy(bf16[256,4,2560]{2,0,1:T(8,128)(2,1)} %bitcast.6) | data formatting | bytes 10485760 | tf_op jit(solution)/shard_map/all_to_all | solution.py:103
  83.8 121.6 %all_to_all.136 = bf16[256,8,1280]{0,2,1:T(8,128)(2,1)} all-to-all(bf16[256,8,1280]{0,2,1:T(8,128)(2,1)} %bitcast.137), channel_id=1, replica_groups=mesh['dp'=4,'fsdp'=8] {'fsdp'}, dimensions={1} | all-to-all | bytes 10485760 | tf_op jit(solution)/shard_map/all_to_all | solution.py:102
  205.4 4.8 all-to-all-start.5
  210.4 14.0 %all_gather.9 = bf16[8,4,1,2048]{3,1,2,0:T(4,128)(2,1)S(1)} all-gather(bf16[1,4,1,2048]{3,1,2,0:T(4,128)(2,1)S(1)} %broadcast_in_dim_reshape.6), channel_id=1, replica_groups=mesh['dp'=4,'fsdp'=8] {'fsdp'}, dimensions={0}, use_global_device_ids=true | all-gather | bytes 147456 | tf_op jit(solution)/shard_map/all_gather | solution.py:115
  224.3 7.8 %copy.53 = bf16[8,256,1280]{2,1,0:T(8,128)(2,1)} copy(bf16[8,256,1280]{1,2,0:T(8,128)(2,1)} %bitcast.136) | data formatting | bytes 10485760 | tf_op jit(solution)/shard_map/all_to_all | solution.py:102
  232.2 4.1 convolution_bitcast_fusion
  236.3 32.0 %reduce-scatter.9.cloned.1.call-done = f32[8,1,1,1280]{3,0,1,2:T(8,128)} async-done(((f32[8,4,1,1280]{3,0,1,2:T(8,128)}), f32[8,1,1,1280]{3,0,1,2:T(8,128)}) %reduce-scatter.9.cloned.1.call-update) | async-done | bytes 40976
  268.2 1.4 copy.54
  269.7 4.6 all-to-all-start.3
  274.3 6.2 copy.59
  280.5 5.2 all-to-all-start.6
  286.4 0.3 copy.72
  286.7 0.3 copy.73
  287.0 0.1 subtract_convert_fusion.1
  287.1 0.1 maximum_bitcast_fusion
  287.2 0.1 fusion.41
  287.3 0.2 fusion.43
  287.5 0.5 fusion.53
  288.0 0.2 fusion.35
  288.2 0.6 fusion.52
  288.8 0.3 fusion.22
  289.2 0.6 copy.57
  289.8 90.0 %all-to-all-done.6 = bf16[256,8,1024]{0,2,1:T(8,128)(2,1)} async-done(((bf16[256,8,1024]{0,2,1:T(8,128)(2,1)}), bf16[256,8,1024]{0,2,1:T(8,128)(2,1)}, u32[]{:S(2)}, u32[]{:S(2)}) %all-to-all-start.6) | async-done | bytes 4194336 | tf_op jit(solution)/shard_map/all_to_all | solution.py:136
  379.8 3.3 all-to-all-start.4
  383.1 6.5 copy.60
  389.6 14.0 %all_gather.10 = bf16[8,4,1,2048]{3,1,2,0:T(4,128)(2,1)S(1)} all-gather(bf16[1,4,1,2048]{3,1,2,0:T(4,128)(2,1)S(1)} %broadcast_in_dim_reshape.7), channel_id=1, replica_groups=mesh['dp'=4,'fsdp'=8] {'fsdp'}, dimensions={0}, use_global_device_ids=true | all-gather | bytes 147456 | tf_op jit(solution)/shard_map/all_gather | solution.py:149
  403.6 3.6 convolution_bitcast_fusion.1
  407.2 23.6 %reduce-scatter.11.cloned.1.call-done = f32[8,1,1,1024]{3,0,1,2:T(8,128)} async-done(((f32[8,4,1,1024]{3,0,1,2:T(8,128)}), f32[8,1,1,1024]{3,0,1,2:T(8,128)}) %reduce-scatter.11.cloned.1.call-update) | async-done | bytes 32784
  430.8 1.4 copy.61
  432.2 4.6 all-to-all-start.7
  436.8 0.2 all-reduce.6.cloned.1.call-start
  437.1 5.5 all-to-all-done.7
  442.6 0.7 multiply_reduce_fusion
  443.9 0.1 convert_bitcast_fusion
  444.0 6.8 copy.62
  450.8 0.5 broadcast.87
  451.3 62.6 %reduce.10 = bf16[8192]{0:T(1024)(128)(2,1)S(1)} reduce(bf16[8192,1,1]{2,1,0:T(2,128)(2,1)} %bitcast.139, bf16[]{:T(256)} %broadcast.87), dimensions={1,2}, to_apply=%bitcast.123.reduce_sub_computation | reduce | bytes 32770
  513.9 7.3 %all_to_all.137 = bf16[4,2,1024]{2,1,0:T(2,128)(2,1)S(1)} all-to-all(bf16[4,2,1024]{2,1,0:T(2,128)(2,1)S(1)} %reshape.331), channel_id=1, replica_groups=mesh['dp'=4,'fsdp'=8] {'dp'}, dimensions={0} | all-to-all | bytes 32768 | tf_op jit(solution)/shard_map/all_to_all | solution.py:157
  521.2 5.6 reshape.332
  526.8 62.0 %bitcast_reduce_fusion = bf16[8192]{0:T(1024)(128)(2,1)S(1)} fusion(bf16[8192,1,1]{2,1,0:T(2,128)(2,1)} %reshape.332), kind=kLoop, calls=%fused_computation.73 | loop fusion | bytes 32768 | tf_op jit(solution)/shard_map/all_to_all | solution.py:157
  588.8 14.2 %all_gather.11 = bf16[8,4,1,2048]{3,1,2,0:T(4,128)(2,1)S(1)} all-gather(bf16[1,4,1,2048]{3,1,2,0:T(4,128)(2,1)S(1)} %broadcast_in_dim.53), channel_id=1, replica_groups=mesh['dp'=4,'fsdp'=8] {'fsdp'}, dimensions={0}, use_global_device_ids=true | all-gather | bytes 147456 | tf_op jit(solution)/shard_map/all_gather | solution.py:158
  603.0 7.6 %fusion.12 = bf16[8,4,1,1,3584]{4,0,1,3,2:T(8,128)(2,1)S(1)} fusion(bf16[2048,3584]{1,0:T(8,128)(2,1)} %param.20, bf16[8,4,1,2048]{3,1,2,0:T(4,128)(2,1)S(1)} %all_gather.11), kind=kOutput, calls=%fused_computation.8 | convolution fusion | flops 469876736 | bytes 15040512 | tf_op jit(solution)/shard_map/fask,kn->fasn/dot_general | solution.py:160
  610.6 7.7 %fusion.15 = bf16[8,4,1,1,3584]{4,0,1,3,2:T(8,128)(2,1)S(1)} fusion(bf16[2048,3584]{1,0:T(8,128)(2,1)} %param.19, bf16[8,4,1,2048]{3,1,2,0:T(4,128)(2,1)S(1)} %all_gather.11), kind=kOutput, calls=%fused_computation.9 | convolution fusion | flops 469876736 | bytes 15040512 | tf_op jit(solution)/shard_map/fask,kn->fasn/dot_general | solution.py:159
  618.3 0.8 pad_maximum_fusion
  619.2 0.6 dynamic-slice.4
  619.8 40.7 %all-reduce.6.cloned.1.call-done = bf16[8,4,1,2,3584]{4,0,1,3,2:T(8,128)(2,1)} async-done(((bf16[8,4,1,2,3584]{4,0,1,3,2:T(8,128)(2,1)}), bf16[8,4,1,2,3584]{4,0,1,3,2:T(8,128)(2,1)}) %all-reduce.6.cloned.1.call-update) | async-done | bytes 458768 | tf_op jit(solution)/shard_map/psum | solution.py:162
  660.5 1.1 convert_element_type.113
  661.6 7.7 %fusion.18 = f32[8,4,1,2048]{3,0,1,2:T(8,128)S(1)} fusion(bf16[3584,2048]{1,0:T(8,128)(2,1)} %param.21, f32[8,4,1,2,3584]{4,0,1,3,2:T(8,128)S(1)} %convert_element_type.113), kind=kOutput, calls=%fused_computation.10 | convolution fusion | flops 470450176 | bytes 15859712 | tf_op jit(solution)/shard_map/fask,kn->fasn/dot_general | solution.py:165
  669.3 0.2 copy.64
  669.5 31.1 %all-reduce.7 = bf16[8,4,1,2048]{3,1,2,0:T(4,128)(2,1)S(1)} all-reduce(f32[8,4,1,2048]{3,1,2,0:T(4,128)S(1)} %copy.64), channel_id=4, replica_groups=mesh['dp'=4,'fsdp'=8] {'fsdp'}, use_global_device_ids=true, to_apply=%region_7.8.clone | all-reduce | flops 65536 | bytes 393216
  700.5 0.7 dynamic-slice_convert_fusion
  701.2 0.7 reduce.11
  702.0 0.6 reshape.333
  702.6 3.3 all-to-all-start.9
  705.9 0.1 maximum_bitcast_fusion.1
  706.0 0.6 copy.101
  706.6 4.0 all-to-all-done.9
  710.6 0.7 fusion.40
  (37 shorter events, 0.4 us)
Async XLA Ops:
  7.2 5.4 copy-start.3
  7.2 5.4 copy-start.2
  7.2 65.4 %all-to-all-start.1 = ((bf16[4,256,2560]{2,1,0:T(8,128)(2,1)}), bf16[4,256,2560]{2,1,0:T(8,128)(2,1)}, u32[]{:S(2)}, u32[]{:S(2)}) async-start(bf16[4,256,2560]{2,1,0:T(8,128)(2,1)} %bitcast.140), calls=%async_computation.1 | async-start | bytes 10485760 | tf_op jit(solution)/shard_map/all_to_all | solution.py:103
  72.5 11.2 %all-to-all-start = ((bf16[1,8,4,256]{3,1,0,2:T(8,128)(2,1)}), bf16[1,8,4,256]{3,1,0,2:T(8,128)(2,1)S(1)}, u32[]{:S(2)}, u32[]{:S(2)}) async-start(bf16[1,8,4,256]{3,1,0,2:T(8,128)(2,1)} %copy.50), calls=%async_computation | async-start | bytes 32768 | tf_op jit(solution)/shard_map/all_to_all | solution.py:109
  205.4 64.3 %all-to-all-start.5 = ((bf16[4,256,2048]{2,1,0:T(8,128)(2,1)}), bf16[4,256,2048]{2,1,0:T(8,128)(2,1)}, u32[]{:S(2)}, u32[]{:S(2)}) async-start(bf16[4,256,2048]{2,1,0:T(8,128)(2,1)} %bitcast.141), calls=%async_computation.5 | async-start | bytes 8388608 | tf_op jit(solution)/shard_map/all_to_all | solution.py:137
  210.3 58.0 %reduce-scatter.9.cloned.1.call-start = ((), (), s32[]{:S(2)}) async-start(), calls=%async_computation.13 | async-start | bytes 204800
  269.7 10.8 %all-to-all-start.3 = ((f32[8,1,1,1280]{3,1,2,0:T(1,128)}), f32[8,1,1,1280]{3,1,2,0:T(1,128)S(1)}, u32[]{:S(2)}, u32[]{:S(2)}) async-start(f32[8,1,1,1280]{3,1,2,0:T(1,128)} %copy.54), calls=%async_computation.3 | async-start | bytes 81920 | tf_op jit(solution)/shard_map/all_to_all | solution.py:120
  280.5 5.9 copy-start
  280.5 6.2 copy-start.1
  280.5 99.3 %all-to-all-start.6 = ((bf16[256,8,1024]{0,2,1:T(8,128)(2,1)}), bf16[256,8,1024]{0,2,1:T(8,128)(2,1)}, u32[]{:S(2)}, u32[]{:S(2)}) async-start(bf16[256,8,1024]{0,2,1:T(8,128)(2,1)} %bitcast.138), calls=%async_computation.6 | async-start | bytes 8388608 | tf_op jit(solution)/shard_map/all_to_all | solution.py:136
  379.8 9.8 %all-to-all-start.4 = ((bf16[1,8,4,256]{3,1,0,2:T(8,128)(2,1)}), bf16[1,8,4,256]{3,1,0,2:T(8,128)(2,1)S(1)}, u32[]{:S(2)}, u32[]{:S(2)}) async-start(bf16[1,8,4,256]{3,1,0,2:T(8,128)(2,1)} %copy.57), calls=%async_computation.4 | async-start | bytes 32768 | tf_op jit(solution)/shard_map/all_to_all | solution.py:143
  383.1 47.8 %reduce-scatter.11.cloned.1.call-start = ((), (), s32[]{:S(2)}) async-start(), calls=%async_computation.14 | async-start | bytes 163840
  389.6 47.5 %copy-start.4 = (bf16[8192]{0:T(1024)(128)(2,1)S(1)}, bf16[8192]{0:T(1024)(128)(2,1)}, u32[]{:S(2)}) copy-start(bf16[8192]{0:T(1024)(128)(2,1)} %param.18) | copy-start | bytes 49156
  432.2 10.3 %all-to-all-start.7 = ((f32[8,1,1,1024]{3,1,2,0:T(1,128)}), f32[8,1,1,1024]{3,1,2,0:T(1,128)S(1)}, u32[]{:S(2)}, u32[]{:S(2)}) async-start(f32[8,1,1,1024]{3,1,2,0:T(1,128)} %copy.61), calls=%async_computation.7 | async-start | bytes 65536 | tf_op jit(solution)/shard_map/all_to_all | solution.py:154
  436.8 223.7 %all-reduce.6.cloned.1.call-start = ((), (), s32[]{:S(2)}) async-start(), calls=%async_computation.12 | async-start | bytes 917504 | tf_op jit(solution)/shard_map/psum | solution.py:162
  610.6 8.5 %copy-start.5 = (u32[32]{0:T(128)S(1)}, u32[32]{0:T(128)}, u32[]{:S(2)}) copy-start(u32[32]{0:T(128)} %constant.44) | copy-start | bytes 388
  702.6 7.9 %all-to-all-start.9 = ((bf16[4,2,1024]{2,1,0:T(2,128)(2,1)}), bf16[4,2,1024]{2,1,0:T(2,128)(2,1)S(1)}, u32[]{:S(2)}, u32[]{:S(2)}) async-start(bf16[4,2,1024]{2,1,0:T(2,128)(2,1)} %reshape.333), calls=%async_computation.9 | async-start | bytes 32768 | tf_op jit(solution)/shard_map/all_to_all | solution.py:170
Sparse Core Ops, SparseCore 0:
  236.4 31.7 reduce-scatter.8
  407.3 23.4 reduce-scatter.10
  619.3 41.1 all-reduce.5
where the time goes:
time: 720 us; the launch traced here: 718 us
  waiting for transfers between devices  254 us (35%)
  blocking collectives  202 us (28%)
  local copies, waits for them, and re-layouts  111 us (15%)
  other arithmetic  68.6 us (10%)
  starting transfers between devices  34.7 us (5%)
  matrix products  31.7 us (4%)
  between operations  16 us (2%)
    all_to_all x1, blocking collectives, on_device(): lax.all_to_all(lax.all_to_all(w_qkv, 'dp', split_axis=0, concat_axis=1, t...  122 us
    all_to_all x1, waiting for transfers between devices, on_device(): lax.all_to_all(lax.all_to_all(w_out, 'dp', split_axis=0, concat_axis=1, t...  90 us
    unnamed x3, other arithmetic  63.4 us
    all_to_all x1, local copies, waits for them, and re-layouts, on_device(): lax.all_to_all(normed_mid[None], 'dp', split_axis=2, concat_axis=0, tiled...  62 us
    all_to_all x1, waiting for transfers between devices, on_device(): lax.all_to_all(w_qkv, 'dp', split_axis=0, concat_axis=1, tiled=True)  57.9 us
    unnamed x5, waiting for transfers between devices  55.7 us
    psum x1, waiting for transfers between devices, on_device(): summed = lax.psum(partials.astype(jnp.bfloat16), 'dp').astype(jnp.float32)  40.7 us
    unnamed x1, blocking collectives  31.1 us
  transfers between devices with their start and end apart: 11, of which 7 were waited for; matrix products, arithmetic and copies ran while one was open for 6% of the time, Pallas kernels for 0%

commit v1 on v0

--- a/solution.py
+++ b/solution.py
@@ -1,6 +1,10 @@
+import functools
+
 import jax
 import jax.numpy as jnp
 from jax import lax
+from jax.experimental import pallas as pl
+from jax.experimental.pallas import tpu as pltpu
 from jax.sharding import PartitionSpec as P
 
 HEADS = 64
@@ -70,16 +74,16 @@
     return mixed.astype(jnp.bfloat16).reshape(seq_count, -1)
 
 
-def quarter_split(values, dp_size, fsdp_size):
-    seq_count = values.shape[0]
-    return values.reshape(seq_count, fsdp_size, dp_size, -1)
-
-
-def quarter_join(moved, dp_size):
-    return moved.reshape(dp_size, moved.shape[0] // dp_size, -1)[None]
-
-
-def on_device(
+def spread_project(rows, weight):
+    block = lax.all_to_all(rows[None], "fsdp", split_axis=2, concat_axis=0, tiled=True)
+    block = lax.all_gather(block, "dp", axis=0)
+    partial_sum = jnp.einsum("afsk,kn->afsn", block, weight, preferred_element_type=jnp.float32)
+    share = lax.psum_scatter(partial_sum, "fsdp", scatter_dimension=1, tiled=True)
+    moved = lax.all_to_all(share, "dp", split_axis=0, concat_axis=3, tiled=True)
+    return moved[0, 0]
+
+
+def on_device_plain(
     hidden_in,
     lengths,
     key_cache,
@@ -95,29 +99,9 @@
     seq_count = hidden_in.shape[0]
     q_width = HEADS * HD
     kv_width = KV_HEADS * HD
-    dp_size = lax.axis_size("dp")
-    fsdp_size = lax.axis_size("fsdp")
     residual = hidden_in.astype(jnp.float32)
     normed = rms_scale(residual, attn_gain).astype(jnp.bfloat16)
-    qkv_tile = lax.all_to_all(
-        lax.all_to_all(w_qkv, "dp", split_axis=0, concat_axis=1, tiled=True),
-        "fsdp",
-        split_axis=1,
-        concat_axis=0,
-        tiled=True,
-    )
-    qkv_moved = lax.all_to_all(
-        quarter_split(normed, dp_size, fsdp_size), "dp", split_axis=2, concat_axis=0, tiled=True
-    )
-    qkv_in = quarter_join(qkv_moved, dp_size)
-    qkv_parts = jnp.einsum(
-        "fpsk,kn->fpsn",
-        lax.all_gather(qkv_in, "fsdp", axis=0, tiled=True),
-        qkv_tile,
-        preferred_element_type=jnp.float32,
-    )
-    qkv_share = lax.psum_scatter(qkv_parts, "dp", scatter_dimension=1, tiled=True)
-    projected = lax.all_to_all(qkv_share, "fsdp", split_axis=0, concat_axis=3, tiled=True)[0, 0]
+    projected = spread_project(normed, w_qkv)
     queries = rotate(projected[:, :q_width].reshape(seq_count, HEADS, HD), lengths).astype(
         jnp.bfloat16
     )
@@ -133,25 +117,7 @@
         value_cache,
         lengths,
     )
-    out_tile = lax.all_to_all(
-        lax.all_to_all(w_out, "dp", split_axis=0, concat_axis=1, tiled=True),
-        "fsdp",
-        split_axis=1,
-        concat_axis=0,
-        tiled=True,
-    )
-    out_moved = lax.all_to_all(
-        quarter_split(mixed, dp_size, fsdp_size), "dp", split_axis=2, concat_axis=0, tiled=True
-    )
-    out_in = quarter_join(out_moved, dp_size)
-    out_parts = jnp.einsum(
-        "fpsk,kn->fpsn",
-        lax.all_gather(out_in, "fsdp", axis=0, tiled=True),
-        out_tile,
-        preferred_element_type=jnp.float32,
-    )
-    out_share = lax.psum_scatter(out_parts, "dp", scatter_dimension=1, tiled=True)
-    attn_sum = lax.all_to_all(out_share, "fsdp", split_axis=0, concat_axis=3, tiled=True)[0, 0]
+    attn_sum = spread_project(mixed, w_out)
     residual_mid = residual + attn_sum
     normed_mid = rms_scale(residual_mid, mlp_gain).astype(jnp.bfloat16)
     mlp_in = lax.all_to_all(normed_mid[None], "dp", split_axis=2, concat_axis=0, tiled=True)
@@ -174,6 +140,454 @@
     return (hidden_out, new_keys.reshape(seq_count, kv_width), new_values)
 
 
+LANES = 128
+MESH = pl.DeviceIdType.MESH
+F32 = jnp.float32
+BF16 = jnp.bfloat16
+
+
+def rms_tile(values, gain):
+    total = jnp.sum(jnp.sum(values * values, axis=1, keepdims=True), axis=0, keepdims=True)
+    return values * lax.rsqrt(total / values.size + norm_eps) * gain.astype(F32)
+
+
+def gather_features(ref, tokens, rows):
+    pieces = [ref[pl.ds(r, tokens, stride=rows), :] for r in range(rows)]
+    return jnp.concatenate(pieces, axis=1).astype(BF16)
+
+
+def layer_kernel(
+    dp_size,
+    fsdp_size,
+    pitch,
+    len_ref,
+    hid_ref,
+    cos_ref,
+    sin_ref,
+    attn_gain_ref,
+    mlp_gain_ref,
+    key_hbm,
+    value_hbm,
+    qkv_hbm,
+    out_hbm,
+    gate_hbm,
+    up_hbm,
+    down_hbm,
+    hidden_ref,
+    keys_ref,
+    values_ref,
+    w_qkv,
+    w_out,
+    w_gate,
+    w_up,
+    w_down,
+    key_buf,
+    value_buf,
+    a_send,
+    a_recv,
+    b_send,
+    b_recv,
+    heads_buf,
+    c_send,
+    c_recv,
+    d_send,
+    d_recv,
+    mid_buf,
+    e_send,
+    e_recv,
+    x_buf,
+    f_send,
+    f_recv,
+    act_buf,
+    h_send,
+    h_recv,
+    load_sem,
+    send_sem,
+    recv_sem,
+):
+    devices = dp_size * fsdp_size
+    my_dp = lax.axis_index("dp")
+    my_fsdp = lax.axis_index("fsdp")
+    me = my_dp * fsdp_size + my_fsdp
+
+    loads = [
+        pltpu.make_async_copy(source, target, load_sem.at[i])
+        for i, (source, target) in enumerate(
+            (
+                (qkv_hbm, w_qkv),
+                (key_hbm.at[0], key_buf),
+                (value_hbm.at[0], value_buf),
+                (out_hbm, w_out),
+                (gate_hbm, w_gate),
+                (up_hbm, w_up),
+                (down_hbm, w_down),
+            )
+        )
+    ]
+    loads[0].start()
+
+    def place(step):
+        other = lax.rem(me + step, devices)
+        return other, other // fsdp_size, lax.rem(other, fsdp_size)
+
+    barrier = pltpu.get_barrier_semaphore()
+
+    @pl.loop(1, devices)
+    def _(step):
+        _, dp_at, fsdp_at = place(step)
+        pl.semaphore_signal(barrier, inc=1, device_id=(dp_at, fsdp_at), device_id_type=MESH)
+
+    def exchange(phase, source, target, rows, offset):
+        mine = pl.ds(pl.multiple_of(me * rows, 8), rows)
+
+        @pl.loop(1, devices)
+        def _(step):
+            other, dp_at, fsdp_at = place(step)
+            start = pl.multiple_of(offset(other, dp_at, fsdp_at) * rows, 8)
+            pltpu.make_async_remote_copy(
+                src_ref=source.at[pl.ds(start, rows)],
+                dst_ref=target.at[mine],
+                send_sem=send_sem.at[phase],
+                recv_sem=recv_sem.at[phase],
+                device_id=(dp_at, fsdp_at),
+                device_id_type=MESH,
+            ).start()
+
+        own = pl.multiple_of(offset(me, my_dp, my_fsdp) * rows, 8)
+        target[mine, :] = source[pl.ds(own, rows), :]
+
+    def wait_all(sem, target, rows):
+        whole = target.at[pl.ds(0, (devices - 1) * rows)]
+        pltpu.make_async_copy(whole, whole, sem).wait()
+
+    def by_fsdp(other, dp_at, fsdp_at):
+        return fsdp_at
+
+    def by_dp(other, dp_at, fsdp_at):
+        return dp_at
+
+    def by_token(other, dp_at, fsdp_at):
+        return other
+
+    def project(x, weight, target, width, step_pitch):
+        chunk = 512
+
+        @pl.loop(0, width // chunk)
+        def _(c):
+            columns = pl.ds(pl.multiple_of(c * chunk, chunk), chunk)
+            result = jnp.dot(x[...], weight[:, columns], preferred_element_type=F32)
+            for j in range(chunk // LANES):
+                row = c * (chunk // LANES) + j
+                target[pl.ds(row, devices, stride=step_pitch), :] = result[
+                    :, j * LANES : (j + 1) * LANES
+                ]
+
+    def sum_block(ref, dp_at, rows, used):
+        total = None
+        for f in range(fsdp_size):
+            start = (dp_at * fsdp_size + f) * rows
+            piece = ref[start : start + used, :]
+            total = piece if total is None else total + piece
+        return total
+
+    residual = hid_ref[...].astype(F32)
+    normed = rms_tile(residual, attn_gain_ref[...])
+    a_send[...] = normed.astype(BF16).astype(F32)
+    row_tiles = a_recv.shape[0] // devices
+    pl.semaphore_wait(barrier, devices - 1)
+    exchange(0, a_send, a_recv, row_tiles, by_fsdp)
+    for i in (1, 2, 3):
+        loads[i].start()
+    loads[0].wait()
+    wait_all(recv_sem.at[0], a_recv, row_tiles)
+    x_rows = row_tiles * LANES
+    x_in = x_buf.at[:, pl.ds(0, x_rows)]
+    x_in[...] = gather_features(a_recv, devices, row_tiles)
+    qkv_width = w_qkv.shape[1]
+    project(x_in, w_qkv, b_send, qkv_width, pitch)
+    exchange(1, b_send, b_recv, pitch, by_token)
+    for i in (4, 5):
+        loads[i].start()
+    wait_all(recv_sem.at[1], b_recv, pitch)
+    used = qkv_width // LANES
+    for d in range(dp_size):
+        heads_buf[d * used : (d + 1) * used, :] = sum_block(b_recv, d, pitch, used)
+
+    def turn(values):
+        return values * cos_ref[...] + pltpu.roll(values, HD // 2, axis=1) * sin_ref[...]
+
+    group = HEADS // KV_HEADS
+    queries = turn(heads_buf[0:HEADS, :]).astype(BF16)
+    new_keys = turn(heads_buf[HEADS : HEADS + KV_HEADS, :]).astype(BF16)
+    new_values = heads_buf[HEADS + KV_HEADS : HEADS + 2 * KV_HEADS, :].astype(BF16)
+    keys_ref[...] = new_keys
+    values_ref[...] = new_values
+    kv_width = KV_HEADS * HD
+    head_of_row = lax.broadcasted_iota(jnp.int32, (HEADS, kv_width), 0) // group
+    head_of_lane = lax.broadcasted_iota(jnp.int32, (HEADS, kv_width), 1) // HD
+    same_head = head_of_row == head_of_lane
+    query_float = queries.astype(F32)
+    wide = jnp.concatenate([query_float] * KV_HEADS, axis=1)
+    wide = jnp.where(same_head, wide, 0.0).astype(BF16)
+    for i in (1, 2):
+        loads[i].wait()
+    scale = HD ** (-0.5)
+    scores = (
+        lax.dot_general(
+            wide, key_buf[...], (((1,), (1,)), ((), ())), preferred_element_type=F32
+        )
+        * scale
+    )
+    position = lax.broadcasted_iota(jnp.int32, scores.shape, 1)
+    scores = jnp.where(position < len_ref[0], scores, -1e30)
+
+    def per_query(rows):
+        spread = jnp.broadcast_to(rows.astype(F32)[:, None, :], (KV_HEADS, group, HD))
+        return spread.reshape(HEADS, HD)
+
+    own_score = jnp.sum(query_float * per_query(new_keys), axis=1, keepdims=True) * scale
+    row_max = jnp.maximum(jnp.max(scores, axis=1, keepdims=True), own_score)
+    weights = jnp.exp(scores - row_max)
+    own_weight = jnp.exp(own_score - row_max)
+    denom_sum = jnp.sum(weights, axis=1, keepdims=True) + own_weight
+    probability = (weights / denom_sum).astype(BF16)
+    own_prob = (own_weight / denom_sum).astype(BF16).astype(F32)
+    mixed_wide = jnp.dot(probability, value_buf[...], preferred_element_type=F32)
+    mixed_wide = jnp.where(same_head, mixed_wide, 0.0)
+    mixed = own_prob * per_query(new_values)
+    for h in range(KV_HEADS):
+        mixed = mixed + mixed_wide[:, h * HD : (h + 1) * HD]
+    c_send[...] = mixed.astype(BF16).astype(F32)
+    exchange(2, c_send, c_recv, row_tiles, by_fsdp)
+    loads[6].start()
+    loads[3].wait()
+    wait_all(recv_sem.at[2], c_recv, row_tiles)
+    x_in[...] = gather_features(c_recv, devices, row_tiles)
+    out_width = w_out.shape[1]
+    out_tiles = out_width // LANES
+    project(x_in, w_out, d_send, out_width, out_tiles)
+    exchange(3, d_send, d_recv, out_tiles, by_token)
+    wait_all(recv_sem.at[3], d_recv, out_tiles)
+    for d in range(dp_size):
+        here = slice(d * out_tiles, (d + 1) * out_tiles)
+        mid_buf[here, :] = hid_ref[here, :].astype(F32) + sum_block(
+            d_recv, d, out_tiles, out_tiles
+        )
+
+    normed_mid = rms_tile(mid_buf[...], mlp_gain_ref[...])
+    e_send[...] = normed_mid.astype(BF16).astype(F32)
+    mid_tiles = e_recv.shape[0] // devices
+    exchange(4, e_send, e_recv, mid_tiles, by_dp)
+    loads[4].wait()
+    loads[5].wait()
+    wait_all(recv_sem.at[4], e_recv, mid_tiles)
+    x_buf[...] = gather_features(e_recv, devices, mid_tiles)
+    part = w_gate.shape[1] // dp_size
+
+    @pl.loop(1, dp_size + 1)
+    def _(step):
+        q = lax.rem(my_dp + step, dp_size)
+        columns = pl.ds(pl.multiple_of(q * part, LANES), part)
+        x = x_buf[...]
+        f_send[q, 0] = jnp.dot(x, w_gate[:, columns], preferred_element_type=F32).astype(BF16)
+        f_send[q, 1] = jnp.dot(x, w_up[:, columns], preferred_element_type=F32).astype(BF16)
+
+        @pl.when(step < dp_size)
+        def _():
+            pltpu.make_async_remote_copy(
+                src_ref=f_send.at[q],
+                dst_ref=f_recv.at[my_dp],
+                send_sem=send_sem.at[5],
+                recv_sem=recv_sem.at[5],
+                device_id=(q, my_fsdp),
+                device_id_type=MESH,
+            ).start()
+
+    def wait_parts(sem, target):
+        whole = target.at[pl.ds(0, dp_size - 1)]
+        pltpu.make_async_copy(whole, whole, sem).wait()
+
+    gate_sum = f_send[my_dp, 0].astype(F32)
+    up_sum = f_send[my_dp, 1].astype(F32)
+    wait_parts(recv_sem.at[5], f_recv)
+    for step in range(1, dp_size):
+        q = lax.rem(my_dp + step, dp_size)
+        gate_sum = gate_sum + f_recv[q, 0].astype(F32)
+        up_sum = up_sum + f_recv[q, 1].astype(F32)
+    act_buf[my_dp] = (gate_sum / (1.0 + jnp.exp(-gate_sum)) * up_sum).astype(BF16)
+
+    @pl.loop(1, dp_size)
+    def _(step):
+        q = lax.rem(my_dp + step, dp_size)
+        pltpu.make_async_remote_copy(
+            src_ref=act_buf.at[my_dp],
+            dst_ref=act_buf.at[my_dp],
+            send_sem=send_sem.at[6],
+            recv_sem=recv_sem.at[6],
+            device_id=(q, my_fsdp),
+            device_id_type=MESH,
+        ).start()
+
+    loads[6].wait()
+    wait_parts(recv_sem.at[6], act_buf)
+    chunk = 512
+
+    @pl.loop(0, out_width // chunk)
+    def _(c):
+        columns = pl.ds(pl.multiple_of(c * chunk, chunk), chunk)
+        result = None
+        for q in range(dp_size):
+            piece = jnp.dot(
+                act_buf[q], w_down[q * part : (q + 1) * part, columns], preferred_element_type=F32
+            )
+            result = piece if result is None else result + piece
+        for j in range(chunk // LANES):
+            row = c * (chunk // LANES) + j
+            h_send[pl.ds(row, devices, stride=out_tiles), :] = result[
+                :, j * LANES : (j + 1) * LANES
+            ]
+
+    exchange(7, h_send, h_recv, out_tiles, by_token)
+    wait_all(recv_sem.at[7], h_recv, out_tiles)
+    for d in range(dp_size):
+        here = slice(d * out_tiles, (d + 1) * out_tiles)
+        down = sum_block(h_recv, d, out_tiles, out_tiles)
+        hidden_ref[here, :] = (mid_buf[here, :] + down).astype(BF16)
+
+    for phase, (target, rows) in enumerate(
+        (
+            (a_recv, row_tiles),
+            (b_recv, pitch),
+            (c_recv, row_tiles),
+            (d_recv, out_tiles),
+            (e_recv, mid_tiles),
+        )
+    ):
+        wait_all(send_sem.at[phase], target, rows)
+    wait_parts(send_sem.at[5], f_send)
+    wait_parts(send_sem.at[6], act_buf)
+    wait_all(send_sem.at[7], h_recv, out_tiles)
+
+
+def on_device(
+    hidden_in,
+    lengths,
+    key_cache,
+    value_cache,
+    attn_gain,
+    w_qkv,
+    w_out,
+    mlp_gain,
+    w_gate,
+    w_up,
+    w_down,
+):
+    dp_size = lax.axis_size("dp")
+    fsdp_size = lax.axis_size("fsdp")
+    devices = dp_size * fsdp_size
+    seq_count, width = hidden_in.shape
+    tile = 8 * LANES
+    if (
+        seq_count != 1
+        or w_qkv.shape[0] % tile
+        or w_out.shape[0] != w_qkv.shape[0]
+        or w_out.shape[1] % tile
+        or w_gate.shape[0] % tile
+        or w_gate.shape[1] % (dp_size * LANES)
+    ):
+        return on_device_plain(
+            hidden_in,
+            lengths,
+            key_cache,
+            value_cache,
+            attn_gain,
+            w_qkv,
+            w_out,
+            mlp_gain,
+            w_gate,
+            w_up,
+            w_down,
+        )
+    half = HD // 2
+    frequency = rope_base ** (-2.0 * jnp.arange(half, dtype=F32) / HD)
+    angles = lengths.astype(F32)[:, None] * frequency[None, :]
+    cosine = jnp.cos(angles)
+    sine = jnp.sin(angles)
+    cosine = jnp.concatenate([cosine, cosine], axis=1)
+    sine = jnp.concatenate([-sine, sine], axis=1)
+    rows = width // LANES
+    context, kv_width = key_cache.shape[1:]
+    row_tiles = w_qkv.shape[0] // LANES
+    out_tiles = w_out.shape[1] // LANES
+    mid_tiles = w_gate.shape[0] // LANES
+    pitch = -(-w_qkv.shape[1] // tile) * 8
+    part = w_gate.shape[1] // dp_size
+    vmem = pl.BlockSpec(memory_space=pltpu.VMEM)
+    anyspace = pl.BlockSpec(memory_space=pl.ANY)
+
+    def tiles(count):
+        return pltpu.VMEM((count, LANES), F32)
+
+    hidden_out, new_keys, new_values = pl.pallas_call(
+        functools.partial(layer_kernel, dp_size, fsdp_size, pitch),
+        out_shape=(
+            jax.ShapeDtypeStruct((rows, LANES), BF16),
+            jax.ShapeDtypeStruct((KV_HEADS, HD), BF16),
+            jax.ShapeDtypeStruct((KV_HEADS, HD), BF16),
+        ),
+        in_specs=[pl.BlockSpec(memory_space=pltpu.SMEM)] + [vmem] * 5 + [anyspace] * 7,
+        out_specs=(vmem, vmem, vmem),
+        scratch_shapes=[
+            pltpu.VMEM(w_qkv.shape, BF16),
+            pltpu.VMEM(w_out.shape, BF16),
+            pltpu.VMEM(w_gate.shape, BF16),
+            pltpu.VMEM(w_up.shape, BF16),
+            pltpu.VMEM(w_down.shape, BF16),
+            pltpu.VMEM((context, kv_width), BF16),
+            pltpu.VMEM((context, kv_width), BF16),
+            tiles(rows),
+            tiles(devices * row_tiles),
+            tiles(devices * pitch),
+            tiles(devices * pitch),
+            tiles(HEADS + 2 * KV_HEADS),
+            tiles(rows),
+            tiles(devices * row_tiles),
+            tiles(devices * out_tiles),
+            tiles(devices * out_tiles),
+            tiles(rows),
+            tiles(rows),
+            tiles(devices * mid_tiles),
+            pltpu.VMEM((devices, max(mid_tiles, row_tiles) * LANES), BF16),
+            pltpu.VMEM((dp_size, 2, devices, part), BF16),
+            pltpu.VMEM((dp_size, 2, devices, part), BF16),
+            pltpu.VMEM((dp_size, devices, part), BF16),
+            tiles(devices * out_tiles),
+            tiles(devices * out_tiles),
+            pltpu.SemaphoreType.DMA((7,)),
+            pltpu.SemaphoreType.DMA((8,)),
+            pltpu.SemaphoreType.DMA((8,)),
+        ],
+        compiler_params=pltpu.CompilerParams(
+            collective_id=0, has_side_effects=True, vmem_limit_bytes=67043328
+        ),
+    )(
+        lengths,
+        hidden_in.reshape(rows, LANES),
+        cosine,
+        sine,
+        attn_gain.reshape(rows, LANES),
+        mlp_gain.reshape(rows, LANES),
+        key_cache,
+        value_cache,
+        w_qkv,
+        w_out,
+        w_gate,
+        w_up,
+        w_down,
+    )
+    return (hidden_out.reshape(1, width), new_keys.reshape(1, kv_width), new_values.reshape(1, kv_width))
+
+
 def solution(mesh):
     in_specs = (
         P(("dp", "fsdp"), None),

time: 720 us -> 80.8 us (0.11)
  waiting for transfers between devices: 254 us -> 0 us
  blocking collectives: 202 us -> 0 us
  local copies, waits for them, and re-layouts: 111 us -> 3.87 us
  Pallas kernels: 0 us -> 72.6 us
  other arithmetic: 68.6 us -> 2.73 us
  starting transfers between devices: 34.7 us -> 0 us
  matrix products: 31.7 us -> 0 us
  between operations: 16 us -> 1.3 us
    all_to_all x8 -> x0, waiting for transfers between devices: 157 us -> none  [the longest x1 90 us: on_device(): lax.all_to_all(lax.all_to_all(w_out, 'dp', split_axis=0, concat_axis=1, t...]
    all_to_all x2 -> x0, blocking collectives: 129 us -> none  [the longest x1 122 us: on_device(): lax.all_to_all(lax.all_to_all(w_qkv, 'dp', split_axis=0, concat_axis=1, t...]
    all_to_all x5 -> x0, local copies, waits for them, and re-layouts: 90.4 us -> none  [the longest x1 62 us: on_device(): lax.all_to_all(normed_mid[None], 'dp', split_axis=2, concat_axis=0, tiled...]
    pallas_call x0 -> x1, Pallas kernels: none -> 72.6 us  [on_device(): pl.pallas_call(functools.partial(layer_kernel, dp_size, fsdp_size, pitch)...]
    unnamed x3 -> x1, other arithmetic: 63.4 us -> 1.45 us
    unnamed x5 -> x0, waiting for transfers between devices: 55.7 us -> none
    all_gather x3 -> x0, blocking collectives: 42.2 us -> none  [the longest x1 14.2 us: on_device(): pieces = lax.all_gather(mlp_in[None], 'fsdp', axis=0, tiled=True)]
    psum x1 -> x0, waiting for transfers between devices: 40.7 us -> none  [on_device(): summed = lax.psum(partials.astype(jnp.bfloat16), 'dp').astype(jnp.float32)]
  transfers between devices with their start and end apart: 11 -> 0, of which waited for: 7 -> 0; matrix products, arithmetic and copies ran while one was open for 6% -> 0% of each run, Pallas kernels for 0% -> 0%
where the time goes in v1:
time: 80.8 us; the launch traced here: 80.5 us
  Pallas kernels  72.6 us (90%)
  local copies, waits for them, and re-layouts  3.87 us (5%)
  other arithmetic  2.73 us (3%)
  between operations  1.3 us (2%)
    pallas_call x1, Pallas kernels, on_device(): pl.pallas_call(functools.partial(layer_kernel, dp_size, fsdp_size, pitch)...  72.6 us
    unnamed x3, local copies, waits for them, and re-layouts  3.87 us

profile of v1, /device:TPU:0, one launch (start us, length us, event | category | flops | bytes accessed | tf_op | source)
XLA Modules:
  0.0 80.5 jit_solution(1683240561429086904)
XLA Ops:
  1.3 0.1 fusion
  1.3 0.1 fusion.2
  1.4 0.6 pad_maximum_fusion.1.sin_ref
  2.0 0.6 pad_maximum_fusion.cos_ref
  2.6 1.5 %reduce = bf16[8192]{0:T(1024)(128)(2,1)} reduce(bf16[1,8192]{1,0:T(2,128)(2,1)} %param.11, bf16[]{:T(256)} %constant.13), dimensions={0}, to_apply=%param.11.reduce_sub_computation | reduce | bytes 32770 | tf_op args[0]
  4.0 72.6 %shard_map.130 = (bf16[64,128]{1,0:T(8,128)(2,1)}, bf16[8,128]{1,0:T(8,128)(2,1)}, bf16[8,128]{1,0:T(8,128)(2,1)}) custom-call(s32[1]{0:T(128)S(6)} %copy.23.len_ref, bf16[64,128]{1,0:T(8,128)(2,1)} %bitcast.19, f32[1,128]{1,0:T(1,128)} %pad_maximum_fusion.cos_ref, f32[1,128]{1,0:T(1,128)} %pad_maximum_fusion.1.sin_ref, bf16[64,128]{1,0:T(8,128)(2,1)} %bitcast.21, ...), custom_call_target="tpu_custom_call" | custom-call | tf_op jit(solution)/shard_map/pallas_call | solution.py:531
  76.6 1.4 %copy.20 = bf16[1,1,64,128]{3,1,2,0:T(2,128)(2,1)} copy(bf16[1,1,64,128]{3,2,1,0:T(8,128)(2,1)} %bitcast.23) | data formatting | bytes 32768
  77.9 1.2 %copy.21 = bf16[1,1,8,128]{3,1,2,0:T(2,128)(2,1)} copy(bf16[1,1,8,128]{3,2,1,0:T(8,128)(2,1)} %bitcast.27) | data formatting | bytes 4096
  79.2 1.3 %copy.22 = bf16[1,1,8,128]{3,1,2,0:T(2,128)(2,1)} copy(bf16[1,1,8,128]{3,2,1,0:T(8,128)(2,1)} %bitcast.26) | data formatting | bytes 4096

commit v2 on v1

--- a/solution.py
+++ b/solution.py
@@ -151,8 +151,10 @@
     return values * lax.rsqrt(total / values.size + norm_eps) * gain.astype(F32)
 
 
-def gather_features(ref, tokens, rows):
-    pieces = [ref[pl.ds(r, tokens, stride=rows), :] for r in range(rows)]
+def gather_features(ref, stage):
+    tokens, rows, _ = ref.shape
+    stage[0 : tokens * rows, :] = ref[...].astype(F32).reshape(tokens * rows, LANES)
+    pieces = [stage[pl.ds(r, tokens, stride=rows), :] for r in range(rows)]
     return jnp.concatenate(pieces, axis=1).astype(BF16)
 
 
@@ -201,6 +203,8 @@
     act_buf,
     h_send,
     h_recv,
+    stage,
+    total_buf,
     load_sem,
     send_sem,
     recv_sem,
@@ -237,24 +241,27 @@
         _, dp_at, fsdp_at = place(step)
         pl.semaphore_signal(barrier, inc=1, device_id=(dp_at, fsdp_at), device_id_type=MESH)
 
-    def exchange(phase, source, target, rows, offset):
-        mine = pl.ds(pl.multiple_of(me * rows, 8), rows)
-
+    def exchange(phase, source, target, offset):
         @pl.loop(1, devices)
         def _(step):
             other, dp_at, fsdp_at = place(step)
-            start = pl.multiple_of(offset(other, dp_at, fsdp_at) * rows, 8)
             pltpu.make_async_remote_copy(
-                src_ref=source.at[pl.ds(start, rows)],
-                dst_ref=target.at[mine],
+                src_ref=source(offset(other, dp_at, fsdp_at)),
+                dst_ref=target(me),
                 send_sem=send_sem.at[phase],
                 recv_sem=recv_sem.at[phase],
                 device_id=(dp_at, fsdp_at),
                 device_id_type=MESH,
             ).start()
 
-        own = pl.multiple_of(offset(me, my_dp, my_fsdp) * rows, 8)
-        target[mine, :] = source[pl.ds(own, rows), :]
+        own = source(offset(me, my_dp, my_fsdp))
+        target(me)[...] = own[...]
+
+    def blocks(ref):
+        return lambda i: ref.at[i]
+
+    def runs(ref, rows):
+        return lambda i: ref.at[pl.ds(pl.multiple_of(i * rows, 8), rows)]
 
     def wait_all(sem, target, rows):
         whole = target.at[pl.ds(0, (devices - 1) * rows)]
@@ -282,6 +289,13 @@
                     :, j * LANES : (j + 1) * LANES
                 ]
 
+    def sum_parts(ref, dp_at):
+        total = None
+        for f in range(fsdp_size):
+            piece = ref[dp_at * fsdp_size + f].astype(F32)
+            total = piece if total is None else total + piece
+        return total
+
     def sum_block(ref, dp_at, rows, used):
         total = None
         for f in range(fsdp_size):
@@ -292,20 +306,20 @@
 
     residual = hid_ref[...].astype(F32)
     normed = rms_tile(residual, attn_gain_ref[...])
-    a_send[...] = normed.astype(BF16).astype(F32)
-    row_tiles = a_recv.shape[0] // devices
+    a_send[...] = normed.astype(BF16).reshape(a_send.shape)
+    row_tiles = a_recv.shape[1]
     pl.semaphore_wait(barrier, devices - 1)
-    exchange(0, a_send, a_recv, row_tiles, by_fsdp)
+    exchange(0, blocks(a_send), blocks(a_recv), by_fsdp)
     for i in (1, 2, 3):
         loads[i].start()
     loads[0].wait()
-    wait_all(recv_sem.at[0], a_recv, row_tiles)
+    wait_all(recv_sem.at[0], a_recv, 1)
     x_rows = row_tiles * LANES
     x_in = x_buf.at[:, pl.ds(0, x_rows)]
-    x_in[...] = gather_features(a_recv, devices, row_tiles)
+    x_in[...] = gather_features(a_recv, stage)
     qkv_width = w_qkv.shape[1]
     project(x_in, w_qkv, b_send, qkv_width, pitch)
-    exchange(1, b_send, b_recv, pitch, by_token)
+    exchange(1, runs(b_send, pitch), runs(b_recv, pitch), by_token)
     for i in (4, 5):
         loads[i].start()
     wait_all(recv_sem.at[1], b_recv, pitch)
@@ -357,31 +371,29 @@
     mixed = own_prob * per_query(new_values)
     for h in range(KV_HEADS):
         mixed = mixed + mixed_wide[:, h * HD : (h + 1) * HD]
-    c_send[...] = mixed.astype(BF16).astype(F32)
-    exchange(2, c_send, c_recv, row_tiles, by_fsdp)
+    c_send[...] = mixed.astype(BF16).reshape(c_send.shape)
+    exchange(2, blocks(c_send), blocks(c_recv), by_fsdp)
     loads[6].start()
     loads[3].wait()
-    wait_all(recv_sem.at[2], c_recv, row_tiles)
-    x_in[...] = gather_features(c_recv, devices, row_tiles)
+    wait_all(recv_sem.at[2], c_recv, 1)
+    x_in[...] = gather_features(c_recv, stage)
     out_width = w_out.shape[1]
     out_tiles = out_width // LANES
-    project(x_in, w_out, d_send, out_width, out_tiles)
-    exchange(3, d_send, d_recv, out_tiles, by_token)
-    wait_all(recv_sem.at[3], d_recv, out_tiles)
+    project(x_in, w_out, stage, out_width, out_tiles)
+    d_send[...] = stage[0 : devices * out_tiles, :].reshape(d_send.shape).astype(BF16)
+    exchange(3, blocks(d_send), blocks(d_recv), by_token)
+    wait_all(recv_sem.at[3], d_recv, 1)
     for d in range(dp_size):
         here = slice(d * out_tiles, (d + 1) * out_tiles)
-        mid_buf[here, :] = hid_ref[here, :].astype(F32) + sum_block(
-            d_recv, d, out_tiles, out_tiles
-        )
+        mid_buf[here, :] = hid_ref[here, :].astype(F32) + sum_parts(d_recv, d)
 
     normed_mid = rms_tile(mid_buf[...], mlp_gain_ref[...])
-    e_send[...] = normed_mid.astype(BF16).astype(F32)
-    mid_tiles = e_recv.shape[0] // devices
-    exchange(4, e_send, e_recv, mid_tiles, by_dp)
+    e_send[...] = normed_mid.astype(BF16).reshape(e_send.shape)
+    exchange(4, blocks(e_send), blocks(e_recv), by_dp)
     loads[4].wait()
     loads[5].wait()
-    wait_all(recv_sem.at[4], e_recv, mid_tiles)
-    x_buf[...] = gather_features(e_recv, devices, mid_tiles)
+    wait_all(recv_sem.at[4], e_recv, 1)
+    x_buf[...] = gather_features(e_recv, stage)
     part = w_gate.shape[1] // dp_size
 
     @pl.loop(1, dp_size + 1)
@@ -423,50 +435,59 @@
             src_ref=act_buf.at[my_dp],
             dst_ref=act_buf.at[my_dp],
             send_sem=send_sem.at[6],
-            recv_sem=recv_sem.at[6],
+            recv_sem=recv_sem.at[7 + step],
             device_id=(q, my_fsdp),
             device_id_type=MESH,
         ).start()
 
     loads[6].wait()
-    wait_parts(recv_sem.at[6], act_buf)
     chunk = 512
-
-    @pl.loop(0, out_width // chunk)
-    def _(c):
-        columns = pl.ds(pl.multiple_of(c * chunk, chunk), chunk)
-        result = None
-        for q in range(dp_size):
-            piece = jnp.dot(
-                act_buf[q], w_down[q * part : (q + 1) * part, columns], preferred_element_type=F32
+    for step in range(dp_size):
+        source = lax.rem(my_dp - step + dp_size, dp_size)
+        if step:
+            block = act_buf.at[0]
+            pltpu.make_async_copy(block, block, recv_sem.at[7 + step]).wait()
+        first, last = step == 0, step == dp_size - 1
+        part_rows = pl.ds(pl.multiple_of(source * part, LANES), part)
+
+        @pl.loop(0, out_width // chunk)
+        def _(c):
+            columns = pl.ds(pl.multiple_of(c * chunk, chunk), chunk)
+            result = jnp.dot(
+                act_buf[source], w_down[part_rows, columns], preferred_element_type=F32
             )
-            result = piece if result is None else result + piece
-        for j in range(chunk // LANES):
-            row = c * (chunk // LANES) + j
-            h_send[pl.ds(row, devices, stride=out_tiles), :] = result[
-                :, j * LANES : (j + 1) * LANES
-            ]
-
-    exchange(7, h_send, h_recv, out_tiles, by_token)
-    wait_all(recv_sem.at[7], h_recv, out_tiles)
+            if not first:
+                result = result + total_buf[c]
+            if not last:
+                total_buf[c] = result
+            else:
+                for j in range(chunk // LANES):
+                    row = c * (chunk // LANES) + j
+                    stage[pl.ds(row, devices, stride=out_tiles), :] = result[
+                        :, j * LANES : (j + 1) * LANES
+                    ]
+
+    h_send[...] = stage[0 : devices * out_tiles, :].reshape(h_send.shape).astype(BF16)
+    exchange(7, blocks(h_send), blocks(h_recv), by_token)
+    wait_all(recv_sem.at[7], h_recv, 1)
     for d in range(dp_size):
         here = slice(d * out_tiles, (d + 1) * out_tiles)
-        down = sum_block(h_recv, d, out_tiles, out_tiles)
+        down = sum_parts(h_recv, d)
         hidden_ref[here, :] = (mid_buf[here, :] + down).astype(BF16)
 
     for phase, (target, rows) in enumerate(
         (
-            (a_recv, row_tiles),
+            (a_recv, 1),
             (b_recv, pitch),
-            (c_recv, row_tiles),
-            (d_recv, out_tiles),
-            (e_recv, mid_tiles),
+            (c_recv, 1),
+            (d_recv, 1),
+            (e_recv, 1),
         )
     ):
         wait_all(send_sem.at[phase], target, rows)
     wait_parts(send_sem.at[5], f_send)
     wait_parts(send_sem.at[6], act_buf)
-    wait_all(send_sem.at[7], h_recv, out_tiles)
+    wait_all(send_sem.at[7], h_recv, 1)
 
 
 def on_device(
@@ -528,6 +549,9 @@
     def tiles(count):
         return pltpu.VMEM((count, LANES), F32)
 
+    def blocks(count, height):
+        return pltpu.VMEM((count, height, LANES), BF16)
+
     hidden_out, new_keys, new_values = pl.pallas_call(
         functools.partial(layer_kernel, dp_size, fsdp_size, pitch),
         out_shape=(
@@ -545,27 +569,29 @@
             pltpu.VMEM(w_down.shape, BF16),
             pltpu.VMEM((context, kv_width), BF16),
             pltpu.VMEM((context, kv_width), BF16),
-            tiles(rows),
-            tiles(devices * row_tiles),
+            blocks(fsdp_size, row_tiles),
+            blocks(devices, row_tiles),
             tiles(devices * pitch),
             tiles(devices * pitch),
             tiles(HEADS + 2 * KV_HEADS),
+            blocks(fsdp_size, row_tiles),
+            blocks(devices, row_tiles),
+            blocks(devices, out_tiles),
+            blocks(devices, out_tiles),
             tiles(rows),
-            tiles(devices * row_tiles),
-            tiles(devices * out_tiles),
-            tiles(devices * out_tiles),
-            tiles(rows),
-            tiles(rows),
-            tiles(devices * mid_tiles),
+            blocks(dp_size, mid_tiles),
+            blocks(devices, mid_tiles),
             pltpu.VMEM((devices, max(mid_tiles, row_tiles) * LANES), BF16),
             pltpu.VMEM((dp_size, 2, devices, part), BF16),
             pltpu.VMEM((dp_size, 2, devices, part), BF16),
             pltpu.VMEM((dp_size, devices, part), BF16),
-            tiles(devices * out_tiles),
-            tiles(devices * out_tiles),
+            blocks(devices, out_tiles),
+            blocks(devices, out_tiles),
+            tiles(devices * max(row_tiles, mid_tiles, out_tiles)),
+            pltpu.VMEM((out_tiles // 4, devices, 4 * LANES), F32),
             pltpu.SemaphoreType.DMA((7,)),
             pltpu.SemaphoreType.DMA((8,)),
-            pltpu.SemaphoreType.DMA((8,)),
+            pltpu.SemaphoreType.DMA((8 + dp_size,)),
         ],
         compiler_params=pltpu.CompilerParams(
             collective_id=0, has_side_effects=True, vmem_limit_bytes=67043328

time: 80.8 us -> 71.9 us (0.89)
  Pallas kernels: 72.6 us -> 63.6 us
    pallas_call x1, Pallas kernels: 72.6 us -> 63.6 us  [on_device(): pl.pallas_call(functools.partial(layer_kernel, dp_size, fsdp_size, pitch)...]
where the time goes in v2:
time: 71.9 us; the launch traced here: 71.5 us
  Pallas kernels  63.6 us (88%)
  local copies, waits for them, and re-layouts  3.87 us (5%)
  other arithmetic  2.73 us (4%)
  between operations  1.3 us (2%)
    pallas_call x1, Pallas kernels, on_device(): pl.pallas_call(functools.partial(layer_kernel, dp_size, fsdp_size, pitch)...  63.6 us
    unnamed x3, local copies, waits for them, and re-layouts  3.87 us
    unnamed x1, other arithmetic  1.45 us

profile of v2, /device:TPU:0, one launch (start us, length us, event | category | flops | bytes accessed | tf_op | source)
XLA Modules:
  0.0 71.5 jit_solution(9632212866592064169)
XLA Ops:
  1.3 0.1 fusion
  1.3 0.1 fusion.2
  1.4 0.6 pad_maximum_fusion.1.sin_ref
  2.0 0.6 pad_maximum_fusion.cos_ref
  2.6 1.5 %reduce = bf16[8192]{0:T(1024)(128)(2,1)} reduce(bf16[1,8192]{1,0:T(2,128)(2,1)} %param.11, bf16[]{:T(256)} %constant.13), dimensions={0}, to_apply=%param.11.reduce_sub_computation | reduce | bytes 32770 | tf_op args[0]
  4.0 63.6 %shard_map.130 = (bf16[64,128]{1,0:T(8,128)(2,1)}, bf16[8,128]{1,0:T(8,128)(2,1)}, bf16[8,128]{1,0:T(8,128)(2,1)}) custom-call(s32[1]{0:T(128)S(6)} %copy.23.len_ref, bf16[64,128]{1,0:T(8,128)(2,1)} %bitcast.19, f32[1,128]{1,0:T(1,128)} %pad_maximum_fusion.cos_ref, f32[1,128]{1,0:T(1,128)} %pad_maximum_fusion.1.sin_ref, bf16[64,128]{1,0:T(8,128)(2,1)} %bitcast.21, ...), custom_call_target="tpu_custom_call" | custom-call | tf_op jit(solution)/shard_map/pallas_call | solution.py:555
  67.6 1.4 %copy.20 = bf16[1,1,64,128]{3,1,2,0:T(2,128)(2,1)} copy(bf16[1,1,64,128]{3,2,1,0:T(8,128)(2,1)} %bitcast.23) | data formatting | bytes 32768
  69.0 1.2 %copy.21 = bf16[1,1,8,128]{3,1,2,0:T(2,128)(2,1)} copy(bf16[1,1,8,128]{3,2,1,0:T(8,128)(2,1)} %bitcast.27) | data formatting | bytes 4096
  70.2 1.3 %copy.22 = bf16[1,1,8,128]{3,1,2,0:T(2,128)(2,1)} copy(bf16[1,1,8,128]{3,2,1,0:T(8,128)(2,1)} %bitcast.26) | data formatting | bytes 4096
